TPU v7x, 256 devices: a whole 4x4x8 slice. The times are simulated.
256 devices in a mesh: wide: 32 (over z, x), narrow: 8 (over y, core).
Axes of the slice: x: 4, y: 4, z: 8, core: 2. Of those that a mesh axis runs over, the one named last changes fastest.
Arguments:
- payload: bfloat16 [1048576, 128], P(('wide', 'narrow')), may hold values from -6 to 6
- first_key: int32 [1048576], P(('wide', 'narrow')), may hold values from 0 to 1073741823
- second_key: int32 [1048576], P(('wide', 'narrow')), may hold values from 0 to 1073741823
- live: int32 [1048576], P(('wide', 'narrow')), may hold values from 0 to 1
- first_bucket: int32 [1048576], P(('wide', 'narrow')), may hold values from 0 to 31, as said below
- second_bucket: int32 [1048576], P(('wide', 'narrow')), may hold values from 0 to 7
Outputs:
- group_mean: bfloat16 [1048576, 128], P(('wide', 'narrow'))
- duplicate_count: int32 [], replicated
Inputs may be any that keep to these rules, and one draw needn't show every extreme that they name: Each device's rows name each pair (first_bucket, second_bucket) exactly 16 times; in every draw there is one bucket pair all of whose rows survive; other rows survive or not as `live` says.
All inputs are finite; a program needn't handle non-finite values.
Results may differ from a plain program's by a relative error of at most 0.001.
Values may be sent and summed in bfloat16 or wider, within the bound.
A program may use at most 64 MiB of HBM per device.

v0:
```python
import jax
import jax.numpy as jnp
from jax import lax
from jax.sharding import Mesh
from jax.sharding import PartitionSpec as P

WIDE = ("wide_0", "wide_1")
NARROW = ("narrow_0", "narrow_1")
WIDE_NARROW = ("wide_0", "wide_1", "narrow_0", "narrow_1")


def in_blocks(array, dim, length):
    lengths = array.shape
    pieces = array.reshape(*lengths[:dim], length, lengths[dim] // length, *lengths[dim + 1 :])
    return jnp.moveaxis(pieces, dim, 0)


def joined_along(pieces, dim):
    lengths = list(pieces.shape[1:])
    lengths[dim] *= pieces.shape[0]
    return jnp.moveaxis(pieces, 0, dim).reshape(lengths)


def joined_exchange(array, axis, axes, splits, concats):
    sizes = [lax.axis_size(a) for a in axes]
    pieces = in_blocks(array, splits[0], sizes[0])
    pieces = jnp.moveaxis(in_blocks(pieces, splits[1] + 1, sizes[1]), 0, 1)
    inside = pieces.shape[2:]
    pieces = pieces.reshape(-1, *inside)
    pieces = lax.all_to_all(pieces, axis, split_axis=0, concat_axis=0, tiled=True)
    pieces = joined_along(pieces.reshape(*sizes, *inside), concats[0] + 1)
    return joined_along(pieces, concats[1])


def by_axis(array, axes):
    for axis in axes:
        array = lax.psum(array, axis)
    return array


def pair_mask(row_one, row_two, row_live, col_one, col_two, col_live):
    return (
        (row_one[:, None] == col_one[None, :])
        & (row_two[:, None] == col_two[None, :])
        & (row_live[:, None] > 0)
        & (col_live[None, :] > 0)
    )


def on_device(payload, first_key, second_key, live, first_bucket, second_bucket):
    wide_count = lax.axis_size(WIDE)
    narrow_count = lax.axis_size(NARROW)
    row_count, feature_cols = payload.shape
    slot_rows = row_count // (wide_count * narrow_count)
    owner = first_bucket * narrow_count + second_bucket
    sort_order = jnp.argsort(owner, stable=True)
    inverse = jnp.argsort(sort_order, stable=True)
    sent_rows = payload[sort_order].reshape(wide_count, narrow_count, slot_rows, feature_cols)
    shaped = (wide_count, narrow_count, slot_rows)
    tags = jnp.stack(
        [
            first_key[sort_order].reshape(shaped),
            second_key[sort_order].reshape(shaped),
            live[sort_order].reshape(shaped),
        ],
        axis=2,
    )
    got_rows, got_tags = (
        joined_exchange(sent_rows, WIDE_NARROW, (WIDE, NARROW), (0, 1), (0, 1)),
        joined_exchange(tags, WIDE_NARROW, (WIDE, NARROW), (0, 1), (0, 1)),
    )
    owner_rows = wide_count * narrow_count * slot_rows
    flat_rows = got_rows.reshape(owner_rows, feature_cols)
    keys_one = got_tags[:, :, 0, :].reshape(owner_rows)
    keys_two = got_tags[:, :, 1, :].reshape(owner_rows)
    alive = got_tags[:, :, 2, :].reshape(owner_rows)
    tile_rows = min(512, owner_rows)
    column_pos = lax.iota(jnp.int32, owner_rows)

    def full_block(block_index, running):
        group_means, duplicate_total = running
        block_start = block_index * tile_rows
        row_one = lax.dynamic_slice_in_dim(keys_one, block_start, tile_rows)
        row_two = lax.dynamic_slice_in_dim(keys_two, block_start, tile_rows)
        row_live = lax.dynamic_slice_in_dim(alive, block_start, tile_rows)
        same = pair_mask(row_one, row_two, row_live, keys_one, keys_two, alive)
        sums = jnp.dot(same.astype(jnp.bfloat16), flat_rows, preferred_element_type=jnp.float32)
        counts = jnp.sum(same.astype(jnp.float32), axis=1)
        row_pos = block_start + lax.iota(jnp.int32, tile_rows)
        earlier = same & (column_pos[None, :] < row_pos[:, None])
        duplicate_total = duplicate_total + jnp.sum(jnp.any(earlier, axis=1).astype(jnp.float32))
        block_mean = (sums / jnp.maximum(counts, 1.0)[:, None]).astype(jnp.bfloat16)
        group_means = lax.dynamic_update_slice_in_dim(group_means, block_mean, block_start, 0)
        return (group_means, duplicate_total)

    start_state = (jnp.zeros((owner_rows, feature_cols), jnp.bfloat16), jnp.zeros((), jnp.float32))
    group_means, duplicate_total = lax.fori_loop(
        0, owner_rows // tile_rows, full_block, start_state
    )
    back_rows = group_means.reshape(wide_count, narrow_count, slot_rows, feature_cols)
    returned = joined_exchange(back_rows, WIDE_NARROW, (WIDE, NARROW), (0, 1), (0, 1))
    group_mean = returned.reshape(row_count, feature_cols)[inverse]
    overall = by_axis(duplicate_total, WIDE_NARROW)
    return (group_mean, overall.astype(jnp.int32))


def solution(mesh):
    torus = Mesh(mesh.devices.reshape(8, 4, 4, 2), ("wide_0", "wide_1", "narrow_0", "narrow_1"))
    return jax.shard_map(
        on_device,
        mesh=torus,
        in_specs=(
            P(WIDE_NARROW, None),
            P(WIDE_NARROW),
            P(WIDE_NARROW),
            P(WIDE_NARROW),
            P(WIDE_NARROW),
            P(WIDE_NARROW),
        ),
        out_specs=(P(WIDE_NARROW, None), P()),
        check_vma=False,
    )
```

profile of v0, /device:TPU:1, one launch (start us, length us, event | category | flops | bytes accessed | tf_op | source)
XLA Modules:
  0.0 323.6 jit_solution(10078858872643697720)
XLA Ops:
  1.5 5.8 %sort.31 = (s32[4096]{0:T(1024)}, s32[4096]{0:T(1024)S(1)}) sort(s32[4096]{0:T(1024)S(1)} %multiply_add_fusion, s32[4096]{0:T(1024)S(1)} %iota.19), dimensions={0}, to_apply=%region_0.0 | sort | flops 49152 | bytes 65536 | tf_op jit(solution)/shard_map/jit(argsort)/sort | solution.py:56
  7.3 23.0 %gather_fusion.2 = s32[4096]{0:T(1024)S(1)} fusion(s32[4096]{0:T(1024)S(1)} %copy-done.1, s32[4096]{0:T(1024)S(1)} %fusion.6), kind=kCustom, calls=%fused_computation.2 | custom fusion | bytes 49152 | tf_op jit(solution)/shard_map/gather | solution.py:64
  30.4 23.0 %gather_fusion.1 = s32[4096]{0:T(1024)S(1)} fusion(s32[4096]{0:T(1024)S(1)} %copy-done.2, s32[4096]{0:T(1024)S(1)} %fusion.6), kind=kCustom, calls=%fused_computation.1 | custom fusion | bytes 49152 | tf_op jit(solution)/shard_map/gather | solution.py:63
  53.4 23.0 %gather_fusion = s32[4096]{0:T(1024)S(1)} fusion(s32[4096]{0:T(1024)S(1)} %copy-done.3, s32[4096]{0:T(1024)S(1)} %fusion.6), kind=kCustom, calls=%fused_computation | custom fusion | bytes 49152 | tf_op jit(solution)/shard_map/gather | solution.py:62
  77.9 15.6 %all-to-all-start = ((s32[256,1,1,3,16]{4,2,3,1,0:T(1,128)}), s32[256,1,1,3,16]{4,2,3,1,0:T(1,128)S(1)}, u32[]{:S(2)}, u32[]{:S(2)}) async-start(s32[256,1,1,3,16]{4,2,3,1,0:T(1,128)} %copy.20), calls=%async_computation | async-start | bytes 786432 | tf_op jit(solution)/shard_map/all_to_all | solution.py:30
  93.6 15.0 %gather_fusion.3 = bf16[4096,128]{1,0:T(8,128)(2,1)} fusion(bf16[4096,128]{1,0:T(8,128)(2,1)S(1)} %copy-done, s32[4096]{0:T(1024)S(1)} %fusion.6), kind=kCustom, calls=%fused_computation.3 | custom fusion | bytes 2113536 | tf_op jit(solution)/shard_map/gather | solution.py:58
  110.7 12.7 %all-to-all-start.1 = ((bf16[256,1,1,16,128]{4,3,2,1,0:T(8,128)(2,1)}), bf16[256,1,1,16,128]{4,3,2,1,0:T(8,128)(2,1)}, u32[]{:S(2)}, u32[]{:S(2)}) async-start(bf16[256,1,1,16,128]{4,3,2,1,0:T(8,128)(2,1)} %bitcast.10), calls=%async_computation.1 | async-start | bytes 2097152 | tf_op jit(solution)/shard_map/all_to_all | solution.py:30
  124.0 28.9 %all-to-all-done.1 = bf16[256,1,1,16,128]{4,3,2,1,0:T(8,128)(2,1)} async-done(((bf16[256,1,1,16,128]{4,3,2,1,0:T(8,128)(2,1)}), bf16[256,1,1,16,128]{4,3,2,1,0:T(8,128)(2,1)}, u32[]{:S(2)}, u32[]{:S(2)}) %all-to-all-start.1) | async-done | bytes 1048608 | tf_op jit(solution)/shard_map/all_to_all | solution.py:30
  154.0 79.1 %while.17 = (s32[]{:T(128)}, bf16[4096,128]{1,0:T(8,128)(2,1)}, f32[]{:T(128)}, s32[4096]{0:T(1024)S(1)}, s32[32,8,1,16]{3,1,0,2:T(8,128)}, /*index=5*/s32[4096]...) while((s32[]{:T(128)}, bf16[4096,128]{1,0:T(8,128)(2,1)}, ...), condition=%wide.wide.region_5.6_spmd.clone, body=%wide.wide.region_1.5_spmd.clone.sunk | while | flops 557979136 | bytes 7565543 | solution.py:97
  154.3 4.1 %fusion.21 = (pred[512]{0:T(512)(128)(4,1)S(1)}, pred[512,4096]{1,0:T(32,128)(4,1)S(1)}) fusion(s32[512]{0:T(512)S(1)} %iota_add_fusion.3, pred[4096]{0:T(1024)(128)(4,1)S(1)} %gt.36, pred[512]{0:T(512)(128)(4,1)S(1)} %dynamic-slice_compare_fusion.3, s32[4096]{0:T(1024)S(1)} %get-tuple-element.400, s32[512]{0:T(512)S(1)} %dynamic_slice.32, ...), kind=kLoop, calls=%fused_computation.9.clone.clone.1 | loop fusion | flops 16776704 | bytes 2141184 | tf_op jit(solution)/shard_map/while/body/eval_jaxpr/reduce_or | solution.py:91
  164.2 4.1 %fusion.21 = (pred[512]{0:T(512)(128)(4,1)S(1)}, pred[512,4096]{1,0:T(32,128)(4,1)S(1)}) fusion(s32[512]{0:T(512)S(1)} %iota_add_fusion.3, pred[4096]{0:T(1024)(128)(4,1)S(1)} %gt.36, pred[512]{0:T(512)(128)(4,1)S(1)} %dynamic-slice_compare_fusion.3, s32[4096]{0:T(1024)S(1)} %get-tuple-element.400, s32[512]{0:T(512)S(1)} %dynamic_slice.32, ...), kind=kLoop, calls=%fused_computation.9.clone.clone.1 | loop fusion | flops 16776704 | bytes 2141184 | tf_op jit(solution)/shard_map/while/body/eval_jaxpr/reduce_or | solution.py:91
  174.1 4.1 %fusion.21 = (pred[512]{0:T(512)(128)(4,1)S(1)}, pred[512,4096]{1,0:T(32,128)(4,1)S(1)}) fusion(s32[512]{0:T(512)S(1)} %iota_add_fusion.3, pred[4096]{0:T(1024)(128)(4,1)S(1)} %gt.36, pred[512]{0:T(512)(128)(4,1)S(1)} %dynamic-slice_compare_fusion.3, s32[4096]{0:T(1024)S(1)} %get-tuple-element.400, s32[512]{0:T(512)S(1)} %dynamic_slice.32, ...), kind=kLoop, calls=%fused_computation.9.clone.clone.1 | loop fusion | flops 16776704 | bytes 2141184 | tf_op jit(solution)/shard_map/while/body/eval_jaxpr/reduce_or | solution.py:91
  184.0 4.1 %fusion.21 = (pred[512]{0:T(512)(128)(4,1)S(1)}, pred[512,4096]{1,0:T(32,128)(4,1)S(1)}) fusion(s32[512]{0:T(512)S(1)} %iota_add_fusion.3, pred[4096]{0:T(1024)(128)(4,1)S(1)} %gt.36, pred[512]{0:T(512)(128)(4,1)S(1)} %dynamic-slice_compare_fusion.3, s32[4096]{0:T(1024)S(1)} %get-tuple-element.400, s32[512]{0:T(512)S(1)} %dynamic_slice.32, ...), kind=kLoop, calls=%fused_computation.9.clone.clone.1 | loop fusion | flops 16776704 | bytes 2141184 | tf_op jit(solution)/shard_map/while/body/eval_jaxpr/reduce_or | solution.py:91
  193.9 4.1 %fusion.21 = (pred[512]{0:T(512)(128)(4,1)S(1)}, pred[512,4096]{1,0:T(32,128)(4,1)S(1)}) fusion(s32[512]{0:T(512)S(1)} %iota_add_fusion.3, pred[4096]{0:T(1024)(128)(4,1)S(1)} %gt.36, pred[512]{0:T(512)(128)(4,1)S(1)} %dynamic-slice_compare_fusion.3, s32[4096]{0:T(1024)S(1)} %get-tuple-element.400, s32[512]{0:T(512)S(1)} %dynamic_slice.32, ...), kind=kLoop, calls=%fused_computation.9.clone.clone.1 | loop fusion | flops 16776704 | bytes 2141184 | tf_op jit(solution)/shard_map/while/body/eval_jaxpr/reduce_or | solution.py:91
  203.8 4.1 %fusion.21 = (pred[512]{0:T(512)(128)(4,1)S(1)}, pred[512,4096]{1,0:T(32,128)(4,1)S(1)}) fusion(s32[512]{0:T(512)S(1)} %iota_add_fusion.3, pred[4096]{0:T(1024)(128)(4,1)S(1)} %gt.36, pred[512]{0:T(512)(128)(4,1)S(1)} %dynamic-slice_compare_fusion.3, s32[4096]{0:T(1024)S(1)} %get-tuple-element.400, s32[512]{0:T(512)S(1)} %dynamic_slice.32, ...), kind=kLoop, calls=%fused_computation.9.clone.clone.1 | loop fusion | flops 16776704 | bytes 2141184 | tf_op jit(solution)/shard_map/while/body/eval_jaxpr/reduce_or | solution.py:91
  213.6 4.1 %fusion.21 = (pred[512]{0:T(512)(128)(4,1)S(1)}, pred[512,4096]{1,0:T(32,128)(4,1)S(1)}) fusion(s32[512]{0:T(512)S(1)} %iota_add_fusion.3, pred[4096]{0:T(1024)(128)(4,1)S(1)} %gt.36, pred[512]{0:T(512)(128)(4,1)S(1)} %dynamic-slice_compare_fusion.3, s32[4096]{0:T(1024)S(1)} %get-tuple-element.400, s32[512]{0:T(512)S(1)} %dynamic_slice.32, ...), kind=kLoop, calls=%fused_computation.9.clone.clone.1 | loop fusion | flops 16776704 | bytes 2141184 | tf_op jit(solution)/shard_map/while/body/eval_jaxpr/reduce_or | solution.py:91
  223.5 4.1 %fusion.21 = (pred[512]{0:T(512)(128)(4,1)S(1)}, pred[512,4096]{1,0:T(32,128)(4,1)S(1)}) fusion(s32[512]{0:T(512)S(1)} %iota_add_fusion.3, pred[4096]{0:T(1024)(128)(4,1)S(1)} %gt.36, pred[512]{0:T(512)(128)(4,1)S(1)} %dynamic-slice_compare_fusion.3, s32[4096]{0:T(1024)S(1)} %get-tuple-element.400, s32[512]{0:T(512)S(1)} %dynamic_slice.32, ...), kind=kLoop, calls=%fused_computation.9.clone.clone.1 | loop fusion | flops 16776704 | bytes 2141184 | tf_op jit(solution)/shard_map/while/body/eval_jaxpr/reduce_or | solution.py:91
  233.0 6.7 %all-to-all-start.2 = ((bf16[256,1,1,16,128]{4,3,2,1,0:T(8,128)(2,1)}), bf16[256,1,1,16,128]{4,3,2,1,0:T(8,128)(2,1)S(1)}, u32[]{:S(2)}, u32[]{:S(2)}) async-start(bf16[256,1,1,16,128]{4,3,2,1,0:T(8,128)(2,1)} %bitcast.66), calls=%async_computation.2 | async-start | bytes 2097152 | tf_op jit(solution)/shard_map/all_to_all | solution.py:30
  239.8 33.2 %psum.28 = f32[]{:T(128)} all-reduce(f32[]{:T(128)} %get-tuple-element.192), channel_id=1, replica_groups=mesh['wide_0'=8,'wide_1'=4,'narrow_0'=4,'narrow_1'=2] {'wide_0'}, use_global_device_ids=true, to_apply=%region_7.8 | all-reduce | flops 1 | bytes 8 | tf_op jit(solution)/shard_map/psum | solution.py:37
  272.9 8.6 %psum.29 = f32[]{:T(128)} all-reduce(f32[]{:T(128)} %psum.28), channel_id=1, replica_groups=mesh['wide_0'=8,'wide_1'=4,'narrow_0'=4,'narrow_1'=2] {'wide_1'}, use_global_device_ids=true, to_apply=%region_8.9 | all-reduce | flops 1 | bytes 8 | tf_op jit(solution)/shard_map/psum | solution.py:37
  281.5 5.8 %sort.32 = (s32[4096]{0:T(1024)}, s32[4096]{0:T(1024)S(1)}) sort(s32[4096]{0:T(1024)S(1)} %get-tuple-element.189, s32[4096]{0:T(1024)S(1)} %iota.21), dimensions={0}, to_apply=%region_6.7 | sort | flops 49152 | bytes 65536 | tf_op jit(solution)/shard_map/jit(argsort)/sort | solution.py:57
  287.3 9.1 %psum.30 = f32[]{:T(128)} all-reduce(f32[]{:T(128)} %psum.29), channel_id=1, replica_groups=mesh['wide_0'=8,'wide_1'=4,'narrow_0'=4,'narrow_1'=2] {'narrow_0'}, use_global_device_ids=true, to_apply=%region_9.10 | all-reduce | flops 1 | bytes 8 | tf_op jit(solution)/shard_map/psum | solution.py:37
  296.5 10.3 %psum.31 = f32[]{:T(128)} all-reduce(f32[]{:T(128)} %psum.30), channel_id=1, replica_groups=mesh['wide_0'=8,'wide_1'=4,'narrow_0'=4,'narrow_1'=2] {'narrow_1'}, use_global_device_ids=true, to_apply=%region_10.11 | all-reduce | flops 1 | bytes 8 | tf_op jit(solution)/shard_map/psum | solution.py:37
  307.5 15.0 %gather_fusion.4 = bf16[4096,128]{1,0:T(8,128)(2,1)} fusion(bf16[4096,128]{1,0:T(8,128)(2,1)S(1)} %bitcast.65, s32[4096]{0:T(1024)S(1)} %fusion.7), kind=kCustom, calls=%fused_computation.4 | custom fusion | bytes 2113536 | tf_op jit(solution)/shard_map/gather | solution.py:102
  (112 shorter events, 46.8 us)
Async XLA Ops:
  0.6 93.0 %copy-start = (bf16[4096,128]{1,0:T(8,128)(2,1)S(1)}, bf16[4096,128]{1,0:T(8,128)(2,1)}, u32[]{:S(2)}) copy-start(bf16[4096,128]{1,0:T(8,128)(2,1)} %param.8) | copy-start | bytes 3145732
  0.6 6.6 %copy-start.1 = (s32[4096]{0:T(1024)S(1)}, s32[4096]{0:T(1024)}, u32[]{:S(2)}) copy-start(s32[4096]{0:T(1024)} %param.11) | copy-start | bytes 49156
  7.3 23.1 %copy-start.2 = (s32[4096]{0:T(1024)S(1)}, s32[4096]{0:T(1024)}, u32[]{:S(2)}) copy-start(s32[4096]{0:T(1024)} %param.10) | copy-start | bytes 49156
  30.3 23.1 %copy-start.3 = (s32[4096]{0:T(1024)S(1)}, s32[4096]{0:T(1024)}, u32[]{:S(2)}) copy-start(s32[4096]{0:T(1024)} %param.9) | copy-start | bytes 49156
  77.9 32.7 %all-to-all-start = ((s32[256,1,1,3,16]{4,2,3,1,0:T(1,128)}), s32[256,1,1,3,16]{4,2,3,1,0:T(1,128)S(1)}, u32[]{:S(2)}, u32[]{:S(2)}) async-start(s32[256,1,1,3,16]{4,2,3,1,0:T(1,128)} %copy.20), calls=%async_computation | async-start | bytes 786432 | tf_op jit(solution)/shard_map/all_to_all | solution.py:30
  110.7 42.2 %all-to-all-start.1 = ((bf16[256,1,1,16,128]{4,3,2,1,0:T(8,128)(2,1)}), bf16[256,1,1,16,128]{4,3,2,1,0:T(8,128)(2,1)}, u32[]{:S(2)}, u32[]{:S(2)}) async-start(bf16[256,1,1,16,128]{4,3,2,1,0:T(8,128)(2,1)} %bitcast.10), calls=%async_computation.1 | async-start | bytes 2097152 | tf_op jit(solution)/shard_map/all_to_all | solution.py:30
  123.4 30.5 %copy-start.4 = (s32[32,8,1,16]{3,1,0,2:T(8,128)}, s32[32,8,1,16]{3,1,0,2:T(8,128)S(1)}, u32[]{:S(2)}) copy-start(s32[32,8,1,16]{3,1,0,2:T(8,128)S(1)} %get-tuple-element.364) | copy-start | bytes 49156
  123.4 30.5 %copy-start.5 = (s32[32,8,1,16]{3,1,0,2:T(8,128)}, s32[32,8,1,16]{3,1,0,2:T(8,128)S(1)}, u32[]{:S(2)}) copy-start(s32[32,8,1,16]{3,1,0,2:T(8,128)S(1)} %get-tuple-element.362) | copy-start | bytes 49156
  233.0 74.4 %all-to-all-start.2 = ((bf16[256,1,1,16,128]{4,3,2,1,0:T(8,128)(2,1)}), bf16[256,1,1,16,128]{4,3,2,1,0:T(8,128)(2,1)S(1)}, u32[]{:S(2)}, u32[]{:S(2)}) async-start(bf16[256,1,1,16,128]{4,3,2,1,0:T(8,128)(2,1)} %bitcast.66), calls=%async_computation.2 | async-start | bytes 2097152 | tf_op jit(solution)/shard_map/all_to_all | solution.py:30
where the time goes:
time: 324 us
  local copies, waits for them, and re-layouts  104 us (32%)
  blocking collectives  61.2 us (19%)
  other arithmetic  59 us (18%)
  starting transfers between devices  35 us (11%)
  waiting for transfers between devices  30.9 us (10%)
  matrix products  25.2 us (8%)
  loops' own time  5.22 us (2%)
    psum x4, blocking collectives, by_axis(): array = lax.psum(array, axis)  61.2 us
    all_to_all x3, starting transfers between devices, joined_exchange(): lax.all_to_all(pieces, axis, split_axis=0, concat_axis=0, tiled=True)  35 us
    reduce_or x8, other arithmetic, full_block(): jnp.any(earlier, axis=1).astype(jnp.float32)  33.1 us
    all_to_all x3, waiting for transfers between devices, joined_exchange(): lax.all_to_all(pieces, axis, split_axis=0, concat_axis=0, tiled=True)  30.9 us
    dot_general x8, matrix products, full_block(): jnp.dot(same.astype(jnp.bfloat16), flat_rows, preferred_element_type=jnp....  25.2 us
    gather x1, local copies, waits for them, and re-layouts, on_device(): live[sort_order].reshape(shaped)  23 us
    gather x1, local copies, waits for them, and re-layouts, on_device(): second_key[sort_order].reshape(shaped)  23 us
    gather x1, local copies, waits for them, and re-layouts, on_device(): first_key[sort_order].reshape(shaped)  23 us
  transfers between devices with their start and end apart: 3, of which 2 were waited for; matrix products, arithmetic and copies ran while one was open for 7% of the time, Pallas kernels for 0%

commit v1 on v0

--- a/solution.py
+++ b/solution.py
@@ -34,7 +34,7 @@
 
 def by_axis(array, axes):
     for axis in axes:
-        array = lax.psum(array, axis)
+        array = jnp.sum(lax.all_gather(array, axis), axis=0)
     return array
 
 

time: 324 us -> 316 us (0.975)
  blocking collectives: 61.2 us -> 50.9 us
  matrix products: 25.2 us -> 15.4 us
  local copies, waits for them, and re-layouts: 104 us -> 113 us
    psum x4 -> x0, blocking collectives: 61.2 us -> none  [by_axis(): array = lax.psum(array, axis)]
    unnamed x0 -> x4, blocking collectives: none -> 50.9 us
    dot_general x8, matrix products: 25.2 us -> 15.4 us  [full_block(): jnp.dot(same.astype(jnp.bfloat16), flat_rows, preferred_element_type=jnp....]
    unnamed x12 -> x32, local copies, waits for them, and re-layouts: 0.03 us -> 8.94 us
  transfers between devices with their start and end apart: 3 -> 3, of which waited for: 2 -> 2; matrix products, arithmetic and copies ran while one was open for 7% -> 10% of each run, Pallas kernels for 0% -> 0%
where the time goes in v1:
time: 316 us
  local copies, waits for them, and re-layouts  113 us (36%)
  other arithmetic  61.9 us (20%)
  blocking collectives  50.9 us (16%)
  starting transfers between devices  34 us (11%)
  waiting for transfers between devices  31.8 us (10%)
  matrix products  15.4 us (5%)
  loops' own time  5.46 us (2%)
    unnamed x4, blocking collectives  50.9 us
    all_to_all x3, starting transfers between devices, joined_exchange(): lax.all_to_all(pieces, axis, split_axis=0, concat_axis=0, tiled=True)  34 us
    reduce_or x8, other arithmetic, full_block(): jnp.any(earlier, axis=1).astype(jnp.float32)  33.1 us
    all_to_all x3, waiting for transfers between devices, joined_exchange(): lax.all_to_all(pieces, axis, split_axis=0, concat_axis=0, tiled=True)  31.8 us
    gather x1, local copies, waits for them, and re-layouts, on_device(): second_key[sort_order].reshape(shaped)  23 us
    gather x1, local copies, waits for them, and re-layouts, on_device(): live[sort_order].reshape(shaped)  23 us
    gather x1, local copies, waits for them, and re-layouts, on_device(): first_key[sort_order].reshape(shaped)  23 us
    dot_general x8, matrix products, full_block(): jnp.dot(same.astype(jnp.bfloat16), flat_rows, preferred_element_type=jnp....  15.4 us
  transfers between devices with their start and end apart: 3, of which 2 were waited for; matrix products, arithmetic and copies ran while one was open for 10% of the time, Pallas kernels for 0%

profile of v1, /device:TPU:1, one launch (start us, length us, event | category | flops | bytes accessed | tf_op | source)
XLA Modules:
  0.0 315.5 jit_solution(14667869075532979340)
XLA Ops:
  1.5 5.8 %sort.31 = (s32[4096]{0:T(1024)}, s32[4096]{0:T(1024)S(1)}) sort(s32[4096]{0:T(1024)S(1)} %multiply_add_fusion, s32[4096]{0:T(1024)S(1)} %iota.19), dimensions={0}, to_apply=%region_0.0 | sort | flops 49152 | bytes 65536 | tf_op jit(solution)/shard_map/jit(argsort)/sort | solution.py:56
  7.3 23.0 %gather_fusion.1 = s32[4096]{0:T(1024)S(1)} fusion(s32[4096]{0:T(1024)S(1)} %copy-done.1, s32[4096]{0:T(1024)S(1)} %fusion.6), kind=kCustom, calls=%fused_computation.1 | custom fusion | bytes 49152 | tf_op jit(solution)/shard_map/gather | solution.py:63
  31.0 23.0 %gather_fusion.2 = s32[4096]{0:T(1024)S(1)} fusion(s32[4096]{0:T(1024)S(1)} %copy-done.2, s32[4096]{0:T(1024)S(1)} %fusion.6), kind=kCustom, calls=%fused_computation.2 | custom fusion | bytes 49152 | tf_op jit(solution)/shard_map/gather | solution.py:64
  54.8 23.0 %gather_fusion = s32[4096]{0:T(1024)S(1)} fusion(s32[4096]{0:T(1024)S(1)} %copy-done.3, s32[4096]{0:T(1024)S(1)} %fusion.6), kind=kCustom, calls=%fused_computation | custom fusion | bytes 49152 | tf_op jit(solution)/shard_map/gather | solution.py:62
  79.1 15.6 %all-to-all-start = ((s32[256,1,1,3,16]{4,2,3,1,0:T(1,128)}), s32[256,1,1,3,16]{4,2,3,1,0:T(1,128)S(1)}, u32[]{:S(2)}, u32[]{:S(2)}) async-start(s32[256,1,1,3,16]{4,2,3,1,0:T(1,128)} %copy.20), calls=%async_computation | async-start | bytes 786432 | tf_op jit(solution)/shard_map/all_to_all | solution.py:30
  94.8 15.0 %gather_fusion.3 = bf16[4096,128]{1,0:T(8,128)(2,1)} fusion(bf16[4096,128]{1,0:T(8,128)(2,1)S(1)} %copy-done, s32[4096]{0:T(1024)S(1)} %fusion.6), kind=kCustom, calls=%fused_computation.3 | custom fusion | bytes 2113536 | tf_op jit(solution)/shard_map/gather | solution.py:58
  111.9 11.7 %all-to-all-start.1 = ((bf16[256,1,1,16,128]{4,3,2,1,0:T(8,128)(2,1)}), bf16[256,1,1,16,128]{4,3,2,1,0:T(8,128)(2,1)S(1)}, u32[]{:S(2)}, u32[]{:S(2)}) async-start(bf16[256,1,1,16,128]{4,3,2,1,0:T(8,128)(2,1)} %bitcast.10), calls=%async_computation.1 | async-start | bytes 2097152 | tf_op jit(solution)/shard_map/all_to_all | solution.py:30
  124.1 29.8 %all-to-all-done.1 = bf16[256,1,1,16,128]{4,3,2,1,0:T(8,128)(2,1)S(1)} async-done(((bf16[256,1,1,16,128]{4,3,2,1,0:T(8,128)(2,1)}), bf16[256,1,1,16,128]{4,3,2,1,0:T(8,128)(2,1)S(1)}, u32[]{:S(2)}, u32[]{:S(2)}) %all-to-all-start.1) | async-done | bytes 1048608 | tf_op jit(solution)/shard_map/all_to_all | solution.py:30
  155.0 69.9 %while.17 = (s32[]{:T(128)}, bf16[4096,128]{1,0:T(8,128)(2,1)}, f32[]{:T(128)}, s32[4096]{0:T(1024)S(1)}, s32[32,8,1,16]{3,1,0,2:T(8,128)}, /*index=5*/s32[4096]...) while((s32[]{:T(128)}, bf16[4096,128]{1,0:T(8,128)(2,1)}, ...), condition=%wide.wide.region_5.6_spmd.clone, body=%wide.wide.region_1.5_spmd.clone.sunk | while | flops 557979136 | bytes 7565543 | solution.py:97
  155.4 4.1 %fusion.21 = (pred[512]{0:T(512)(128)(4,1)S(1)}, pred[512,4096]{1,0:T(32,128)(4,1)S(1)}) fusion(s32[512]{0:T(512)S(1)} %iota_add_fusion.3, pred[4096]{0:T(1024)(128)(4,1)S(1)} %gt.36, pred[512]{0:T(512)(128)(4,1)S(1)} %dynamic-slice_compare_fusion.3, s32[4096]{0:T(1024)S(1)} %get-tuple-element.400, s32[512]{0:T(512)S(1)} %dynamic_slice.32, ...), kind=kLoop, calls=%fused_computation.9.clone.clone.1 | loop fusion | flops 16776704 | bytes 2141184 | tf_op jit(solution)/shard_map/while/body/eval_jaxpr/reduce_or | solution.py:91
  164.2 4.1 %fusion.21 = (pred[512]{0:T(512)(128)(4,1)S(1)}, pred[512,4096]{1,0:T(32,128)(4,1)S(1)}) fusion(s32[512]{0:T(512)S(1)} %iota_add_fusion.3, pred[4096]{0:T(1024)(128)(4,1)S(1)} %gt.36, pred[512]{0:T(512)(128)(4,1)S(1)} %dynamic-slice_compare_fusion.3, s32[4096]{0:T(1024)S(1)} %get-tuple-element.400, s32[512]{0:T(512)S(1)} %dynamic_slice.32, ...), kind=kLoop, calls=%fused_computation.9.clone.clone.1 | loop fusion | flops 16776704 | bytes 2141184 | tf_op jit(solution)/shard_map/while/body/eval_jaxpr/reduce_or | solution.py:91
  172.9 4.1 %fusion.21 = (pred[512]{0:T(512)(128)(4,1)S(1)}, pred[512,4096]{1,0:T(32,128)(4,1)S(1)}) fusion(s32[512]{0:T(512)S(1)} %iota_add_fusion.3, pred[4096]{0:T(1024)(128)(4,1)S(1)} %gt.36, pred[512]{0:T(512)(128)(4,1)S(1)} %dynamic-slice_compare_fusion.3, s32[4096]{0:T(1024)S(1)} %get-tuple-element.400, s32[512]{0:T(512)S(1)} %dynamic_slice.32, ...), kind=kLoop, calls=%fused_computation.9.clone.clone.1 | loop fusion | flops 16776704 | bytes 2141184 | tf_op jit(solution)/shard_map/while/body/eval_jaxpr/reduce_or | solution.py:91
  181.6 4.1 %fusion.21 = (pred[512]{0:T(512)(128)(4,1)S(1)}, pred[512,4096]{1,0:T(32,128)(4,1)S(1)}) fusion(s32[512]{0:T(512)S(1)} %iota_add_fusion.3, pred[4096]{0:T(1024)(128)(4,1)S(1)} %gt.36, pred[512]{0:T(512)(128)(4,1)S(1)} %dynamic-slice_compare_fusion.3, s32[4096]{0:T(1024)S(1)} %get-tuple-element.400, s32[512]{0:T(512)S(1)} %dynamic_slice.32, ...), kind=kLoop, calls=%fused_computation.9.clone.clone.1 | loop fusion | flops 16776704 | bytes 2141184 | tf_op jit(solution)/shard_map/while/body/eval_jaxpr/reduce_or | solution.py:91
  190.4 4.1 %fusion.21 = (pred[512]{0:T(512)(128)(4,1)S(1)}, pred[512,4096]{1,0:T(32,128)(4,1)S(1)}) fusion(s32[512]{0:T(512)S(1)} %iota_add_fusion.3, pred[4096]{0:T(1024)(128)(4,1)S(1)} %gt.36, pred[512]{0:T(512)(128)(4,1)S(1)} %dynamic-slice_compare_fusion.3, s32[4096]{0:T(1024)S(1)} %get-tuple-element.400, s32[512]{0:T(512)S(1)} %dynamic_slice.32, ...), kind=kLoop, calls=%fused_computation.9.clone.clone.1 | loop fusion | flops 16776704 | bytes 2141184 | tf_op jit(solution)/shard_map/while/body/eval_jaxpr/reduce_or | solution.py:91
  199.1 4.1 %fusion.21 = (pred[512]{0:T(512)(128)(4,1)S(1)}, pred[512,4096]{1,0:T(32,128)(4,1)S(1)}) fusion(s32[512]{0:T(512)S(1)} %iota_add_fusion.3, pred[4096]{0:T(1024)(128)(4,1)S(1)} %gt.36, pred[512]{0:T(512)(128)(4,1)S(1)} %dynamic-slice_compare_fusion.3, s32[4096]{0:T(1024)S(1)} %get-tuple-element.400, s32[512]{0:T(512)S(1)} %dynamic_slice.32, ...), kind=kLoop, calls=%fused_computation.9.clone.clone.1 | loop fusion | flops 16776704 | bytes 2141184 | tf_op jit(solution)/shard_map/while/body/eval_jaxpr/reduce_or | solution.py:91
  207.9 4.1 %fusion.21 = (pred[512]{0:T(512)(128)(4,1)S(1)}, pred[512,4096]{1,0:T(32,128)(4,1)S(1)}) fusion(s32[512]{0:T(512)S(1)} %iota_add_fusion.3, pred[4096]{0:T(1024)(128)(4,1)S(1)} %gt.36, pred[512]{0:T(512)(128)(4,1)S(1)} %dynamic-slice_compare_fusion.3, s32[4096]{0:T(1024)S(1)} %get-tuple-element.400, s32[512]{0:T(512)S(1)} %dynamic_slice.32, ...), kind=kLoop, calls=%fused_computation.9.clone.clone.1 | loop fusion | flops 16776704 | bytes 2141184 | tf_op jit(solution)/shard_map/while/body/eval_jaxpr/reduce_or | solution.py:91
  216.6 4.1 %fusion.21 = (pred[512]{0:T(512)(128)(4,1)S(1)}, pred[512,4096]{1,0:T(32,128)(4,1)S(1)}) fusion(s32[512]{0:T(512)S(1)} %iota_add_fusion.3, pred[4096]{0:T(1024)(128)(4,1)S(1)} %gt.36, pred[512]{0:T(512)(128)(4,1)S(1)} %dynamic-slice_compare_fusion.3, s32[4096]{0:T(1024)S(1)} %get-tuple-element.400, s32[512]{0:T(512)S(1)} %dynamic_slice.32, ...), kind=kLoop, calls=%fused_computation.9.clone.clone.1 | loop fusion | flops 16776704 | bytes 2141184 | tf_op jit(solution)/shard_map/while/body/eval_jaxpr/reduce_or | solution.py:91
  225.0 6.7 %all-to-all-start.2 = ((bf16[256,1,1,16,128]{4,3,2,1,0:T(8,128)(2,1)}), bf16[256,1,1,16,128]{4,3,2,1,0:T(8,128)(2,1)S(1)}, u32[]{:S(2)}, u32[]{:S(2)}) async-start(bf16[256,1,1,16,128]{4,3,2,1,0:T(8,128)(2,1)} %bitcast.16), calls=%async_computation.2 | async-start | bytes 2097152 | tf_op jit(solution)/shard_map/all_to_all | solution.py:30
  231.8 5.8 %sort.32 = (s32[4096]{0:T(1024)}, s32[4096]{0:T(1024)S(1)}) sort(s32[4096]{0:T(1024)S(1)} %get-tuple-element.189, s32[4096]{0:T(1024)S(1)} %iota.21), dimensions={0}, to_apply=%region_6.7 | sort | flops 49152 | bytes 65536 | tf_op jit(solution)/shard_map/jit(argsort)/sort | solution.py:57
  239.6 24.9 %all-reduce = f32[8]{0:T(128)S(1)} all-reduce(f32[8]{0:T(128)S(1)} %dynamic-update-slice), channel_id=1, replica_groups=mesh['wide_0'=8,'wide_1'=4,'narrow_0'=4,'narrow_1'=2] {'wide_0'}, use_global_device_ids=true, to_apply=%add | all-reduce | flops 8 | bytes 64
  267.1 8.0 %all-reduce.1 = f32[4]{0:T(128)S(1)} all-reduce(f32[4]{0:T(128)S(1)} %dynamic-update-slice.1), channel_id=1, replica_groups=mesh['wide_0'=8,'wide_1'=4,'narrow_0'=4,'narrow_1'=2] {'wide_1'}, use_global_device_ids=true, to_apply=%add.1 | all-reduce | flops 4 | bytes 32
  277.8 8.5 %all-reduce.2 = f32[4]{0:T(128)S(1)} all-reduce(f32[4]{0:T(128)S(1)} %dynamic-update-slice.2), channel_id=1, replica_groups=mesh['wide_0'=8,'wide_1'=4,'narrow_0'=4,'narrow_1'=2] {'narrow_0'}, use_global_device_ids=true, to_apply=%add.2 | all-reduce | flops 4 | bytes 32
  288.4 9.6 %all-reduce.3 = f32[2]{0:T(128)S(1)} all-reduce(f32[2]{0:T(128)S(1)} %dynamic-update-slice.3), channel_id=1, replica_groups=mesh['wide_0'=8,'wide_1'=4,'narrow_0'=4,'narrow_1'=2] {'narrow_1'}, use_global_device_ids=true, to_apply=%add.3 | all-reduce | flops 2 | bytes 16
  299.4 15.0 %gather_fusion.4 = bf16[4096,128]{1,0:T(8,128)(2,1)} fusion(bf16[4096,128]{1,0:T(8,128)(2,1)S(1)} %bitcast.73, s32[4096]{0:T(1024)S(1)} %fusion.7), kind=kCustom, calls=%fused_computation.4 | custom fusion | bytes 2113536 | tf_op jit(solution)/shard_map/gather | solution.py:102
  (136 shorter events, 48.8 us)
Async XLA Ops:
  0.6 94.1 %copy-start = (bf16[4096,128]{1,0:T(8,128)(2,1)S(1)}, bf16[4096,128]{1,0:T(8,128)(2,1)}, u32[]{:S(2)}) copy-start(bf16[4096,128]{1,0:T(8,128)(2,1)} %param.8) | copy-start | bytes 3145732
  0.6 6.6 %copy-start.1 = (s32[4096]{0:T(1024)S(1)}, s32[4096]{0:T(1024)}, u32[]{:S(2)}) copy-start(s32[4096]{0:T(1024)} %param.10) | copy-start | bytes 49156
  30.3 0.7 copy-start.2
  54.1 0.7 copy-start.3
  79.1 32.7 %all-to-all-start = ((s32[256,1,1,3,16]{4,2,3,1,0:T(1,128)}), s32[256,1,1,3,16]{4,2,3,1,0:T(1,128)S(1)}, u32[]{:S(2)}, u32[]{:S(2)}) async-start(s32[256,1,1,3,16]{4,2,3,1,0:T(1,128)} %copy.20), calls=%async_computation | async-start | bytes 786432 | tf_op jit(solution)/shard_map/all_to_all | solution.py:30
  111.9 42.1 %all-to-all-start.1 = ((bf16[256,1,1,16,128]{4,3,2,1,0:T(8,128)(2,1)}), bf16[256,1,1,16,128]{4,3,2,1,0:T(8,128)(2,1)S(1)}, u32[]{:S(2)}, u32[]{:S(2)}) async-start(bf16[256,1,1,16,128]{4,3,2,1,0:T(8,128)(2,1)} %bitcast.10), calls=%async_computation.1 | async-start | bytes 2097152 | tf_op jit(solution)/shard_map/all_to_all | solution.py:30
  123.6 31.4 %copy-start.4 = (s32[32,8,1,16]{3,1,0,2:T(8,128)}, s32[32,8,1,16]{3,1,0,2:T(8,128)S(1)}, u32[]{:S(2)}) copy-start(s32[32,8,1,16]{3,1,0,2:T(8,128)S(1)} %get-tuple-element.364) | copy-start | bytes 49156
  123.6 31.4 %copy-start.5 = (s32[32,8,1,16]{3,1,0,2:T(8,128)}, s32[32,8,1,16]{3,1,0,2:T(8,128)S(1)}, u32[]{:S(2)}) copy-start(s32[32,8,1,16]{3,1,0,2:T(8,128)S(1)} %get-tuple-element.362) | copy-start | bytes 49156
  225.0 12.6 %copy-start.9 = (u32[256]{0:T(256)S(1)}, u32[256]{0:T(256)}, u32[]{:S(2)}) copy-start(u32[256]{0:T(256)} %constant.61) | copy-start | bytes 3076
  225.0 13.9 %copy-start.8 = (u32[256]{0:T(256)S(1)}, u32[256]{0:T(256)}, u32[]{:S(2)}) copy-start(u32[256]{0:T(256)} %constant.66) | copy-start | bytes 3076
  225.0 41.5 %copy-start.7 = (u32[256]{0:T(256)S(1)}, u32[256]{0:T(256)}, u32[]{:S(2)}) copy-start(u32[256]{0:T(256)} %constant.71) | copy-start | bytes 3076
  225.0 52.2 %copy-start.6 = (u32[256]{0:T(256)S(1)}, u32[256]{0:T(256)}, u32[]{:S(2)}) copy-start(u32[256]{0:T(256)} %constant.76) | copy-start | bytes 3076
  225.0 74.4 %all-to-all-start.2 = ((bf16[256,1,1,16,128]{4,3,2,1,0:T(8,128)(2,1)}), bf16[256,1,1,16,128]{4,3,2,1,0:T(8,128)(2,1)S(1)}, u32[]{:S(2)}, u32[]{:S(2)}) async-start(bf16[256,1,1,16,128]{4,3,2,1,0:T(8,128)(2,1)} %bitcast.16), calls=%async_computation.2 | async-start | bytes 2097152 | tf_op jit(solution)/shard_map/all_to_all | solution.py:30
